TPU v7x, 16 devices: a 4x2x1 block of a 4x4x8 slice. The times are simulated.
16 devices in a mesh: rep: 2 (over y, z), pp: 8 (over x, core).
Axes of the slice: x: 4, y: 2, z: 1, core: 2. Of those that a mesh axis runs over, the one named last changes fastest.
The devices are a block of a 4x4x8 slice.
Arguments:
- x: bfloat16 [32, 512, 512], P('rep'), parts along dimension 0
- dy: bfloat16 [32, 512, 512], P('rep'), parts along dimension 0
- w_gate: bfloat16 [8, 512, 1408], P('pp')
- w_up: bfloat16 [8, 512, 1408], P('pp')
- w_down: bfloat16 [8, 1408, 512], P('pp')
Outputs:
- output 1: bfloat16 [16, 512, 1408], P(('rep', 'pp')), parts along dimension 0
- output 2: bfloat16 [16, 512, 1408], P(('rep', 'pp')), parts along dimension 0
- output 3: bfloat16 [16, 1408, 512], P(('rep', 'pp')), parts along dimension 0
There are 2 independent parts. A program takes and returns all parts, laid end to end along the dimension named above; an argument that names none is the same for every part.
All inputs are finite; a program needn't handle non-finite values.
Results may differ from a plain program's by a relative error of at most 0.0298.
Values are sent between devices in bfloat16 or wider.
A program may use at most 768 MiB of HBM per device.

v0:
```python
import jax
import jax.numpy as jnp
from jax import lax
from jax.sharding import PartitionSpec as P

NAMES = ("w_gate", "w_up", "w_down")


def matmul(a, w):
    return jnp.dot(a, w, preferred_element_type=jnp.float32).astype(jnp.bfloat16)


def normed(h):
    wide = h.astype(jnp.float32)
    scale = lax.rsqrt(jnp.mean(wide**2, -1, keepdims=True) + 1e-6)
    return (wide * scale).astype(jnp.bfloat16)


def layer(h, w):
    a = normed(h)
    gate = jnp.dot(a, w["w_gate"], preferred_element_type=jnp.float32)
    up = jnp.dot(a, w["w_up"], preferred_element_type=jnp.float32)
    return h + matmul((jax.nn.silu(gate) * up).astype(jnp.bfloat16), w["w_down"])


def stage(weights, h):
    for number in range(weights["w_gate"].shape[0]):
        h = layer(h, {name: w[number] for name, w in weights.items()})
    return h


def solution(mesh):
    stages = mesh.shape["pp"]
    onward = [(i, i + 1) for i in range(stages - 1)]
    back_again = [(i + 1, i) for i in range(stages - 1)]

    def step(x, dy, *arrays):
        weights = dict(zip(NAMES, arrays, strict=True))
        micro, me = x.shape[0], lax.axis_index("pp")
        kept, came = jnp.zeros_like(x), jnp.zeros_like(x[0])
        for t in range(micro + stages - 1):
            number = jnp.clip(t - me, 0, micro - 1)
            at_work = (t >= me) & (t - me < micro)
            h = jnp.where(me == 0, x[min(t, micro - 1)], came)
            was = lax.dynamic_index_in_dim(kept, number, 0, keepdims=False)
            kept = lax.dynamic_update_index_in_dim(kept, jnp.where(at_work, h, was), number, 0)
            came = lax.ppermute(stage(weights, h), "pp", onward)
        total = {name: jnp.zeros(w.shape, jnp.float32) for name, w in weights.items()}
        came, behind = jnp.zeros_like(x[0]), stages - 1 - me
        for t in range(micro + stages - 1):
            number = jnp.clip(t - behind, 0, micro - 1)
            at_work = (t >= behind) & (t - behind < micro)
            by_y = jnp.where(behind == 0, dy[min(t, micro - 1)], came)
            _, back = jax.vjp(stage, weights, lax.dynamic_index_in_dim(kept, number, 0, keepdims=False))
            by_w, by_h = back(by_y)
            total = {name: total[name] + jnp.where(at_work, by_w[name].astype(jnp.float32), 0.0) for name in NAMES}
            came = lax.ppermute(by_h, "pp", back_again)
        return tuple(total[name].astype(jnp.bfloat16) for name in NAMES)

    return jax.shard_map(
        step,
        mesh=mesh,
        in_specs=(P("rep", None, None),) * 2 + (P("pp", None, None),) * 3,
        out_specs=(P(("rep", "pp"), None, None),) * 3,
        check_vma=False,
    )
```

profile of v0, /device:TPU:113, one launch (start us, length us, event | category | flops | bytes accessed | tf_op | source)
XLA Modules:
  0.0 1030.1 jit_solution(5561721897027467204)
XLA Ops:
  15.7 6.1 collective-permute-done
  25.7 5.4 fusion.1034
  35.5 6.1 collective-permute-done.1
  45.5 5.3 fusion.1031
  55.3 6.1 collective-permute-done.2
  66.1 5.6 fusion.1028
  76.3 5.9 collective-permute-done.3
  86.9 5.6 fusion.1025
  96.9 6.1 collective-permute-done.4
  107.8 5.6 fusion.1022
  117.8 6.1 collective-permute-done.5
  128.6 5.6 fusion.1019
  138.6 6.1 collective-permute-done.6
  149.4 5.6 fusion.1016
  159.8 5.7 collective-permute-done.7
  170.2 5.6 fusion.1013
  180.3 6.1 collective-permute-done.8
  191.1 5.6 fusion.1010
  201.1 6.0 collective-permute-done.9
  274.6 5.3 fusion.998
  295.3 5.3 fusion.995
  357.4 5.3 fusion.986
  378.1 5.3 fusion.983
  1005.0 24.6 %fusion.305 = bf16[1,1408,512]{2,1,0:T(8,128)(2,1)} fusion(f32[1408,512]{1,0:T(8,128)} %fusion.68, f32[1408,512]{1,0:T(8,128)} %fusion.66, f32[1408,512]{1,0:T(8,128)} %fusion.64, f32[1408,512]{1,0:T(8,128)} %fusion.62, f32[1408,512]{1,0:T(8,128)} %fusion.60, f32[1408,512]{1,0:T(8,128)} %fusion.58, f32[1408,512]{1,0:T(8,128)} %fusion.56, ...), kind=kOutput, calls=%fused_computation.531 | convolution fusion | flops 761266176 | bytes 71172096 | tf_op jit(solution)/shard_map/transpose(jvp())/dot_general | solution.py:10
  (570 shorter events, 870.7 us)
Async XLA Ops:
  11.1 10.7 %collective-permute-start = (bf16[512,512]{1,0:T(8,128)(2,1)}, bf16[512,512]{1,0:T(8,128)(2,1)S(1)}, u32[]{:S(2)}, u32[]{:S(2)}) collective-permute-start(bf16[512,512]{1,0:T(8,128)(2,1)} %fusion.1037), channel_id=1, source_target_pairs={{0,1},{1,2},{2,3},{3,4},{4,5},{5,6},{6,7},{8,9},{9,10},{10,11},{11... | collective-permute-start | bytes 1572872 | tf_op jit(solution)/shard_map/ppermute | solution.py:47
  217.3 13.7 %collective-permute-start.10 = (bf16[512,512]{1,0:T(8,128)(2,1)}, bf16[512,512]{1,0:T(8,128)(2,1)S(1)}, u32[]{:S(2)}, u32[]{:S(2)}) collective-permute-start(bf16[512,512]{1,0:T(8,128)(2,1)} %fusion.1007), channel_id=1, source_target_pairs={{0,1},{1,2},{2,3},{3,4},{4,5},{5,6},{6,7},{8,9},{9,10},{10,11},{11... | collective-permute-start | bytes 1572872 | tf_op jit(solution)/shard_map/ppermute | solution.py:47
  259.2 10.7 %collective-permute-start.12 = (bf16[512,512]{1,0:T(8,128)(2,1)}, bf16[512,512]{1,0:T(8,128)(2,1)S(1)}, u32[]{:S(2)}, u32[]{:S(2)}) collective-permute-start(bf16[512,512]{1,0:T(8,128)(2,1)} %fusion.1001), channel_id=1, source_target_pairs={{0,1},{1,2},{2,3},{3,4},{4,5},{5,6},{6,7},{8,9},{9,10},{10,11},{11... | collective-permute-start | bytes 1572872 | tf_op jit(solution)/shard_map/ppermute | solution.py:47
  279.9 10.6 %collective-permute-start.13 = (bf16[512,512]{1,0:T(8,128)(2,1)}, bf16[512,512]{1,0:T(8,128)(2,1)S(1)}, u32[]{:S(2)}, u32[]{:S(2)}) collective-permute-start(bf16[512,512]{1,0:T(8,128)(2,1)} %fusion.998), channel_id=1, source_target_pairs={{0,1},{1,2},{2,3},{3,4},{4,5},{5,6},{6,7},{8,9},{9,10},{10,11},{11... | collective-permute-start | bytes 1572872 | tf_op jit(solution)/shard_map/ppermute | solution.py:47
  300.6 10.6 %collective-permute-start.14 = (bf16[512,512]{1,0:T(8,128)(2,1)}, bf16[512,512]{1,0:T(8,128)(2,1)S(1)}, u32[]{:S(2)}, u32[]{:S(2)}) collective-permute-start(bf16[512,512]{1,0:T(8,128)(2,1)} %fusion.995), channel_id=1, source_target_pairs={{0,1},{1,2},{2,3},{3,4},{4,5},{5,6},{6,7},{8,9},{9,10},{10,11},{11... | collective-permute-start | bytes 1572872 | tf_op jit(solution)/shard_map/ppermute | solution.py:47
  321.3 10.9 %collective-permute-start.15 = (bf16[512,512]{1,0:T(8,128)(2,1)}, bf16[512,512]{1,0:T(8,128)(2,1)S(1)}, u32[]{:S(2)}, u32[]{:S(2)}) collective-permute-start(bf16[512,512]{1,0:T(8,128)(2,1)} %fusion.992), channel_id=1, source_target_pairs={{0,1},{1,2},{2,3},{3,4},{4,5},{5,6},{6,7},{8,9},{9,10},{10,11},{11... | collective-permute-start | bytes 1572872 | tf_op jit(solution)/shard_map/ppermute | solution.py:47
  362.6 10.6 %collective-permute-start.17 = (bf16[512,512]{1,0:T(8,128)(2,1)}, bf16[512,512]{1,0:T(8,128)(2,1)S(1)}, u32[]{:S(2)}, u32[]{:S(2)}) collective-permute-start(bf16[512,512]{1,0:T(8,128)(2,1)} %fusion.986), channel_id=1, source_target_pairs={{0,1},{1,2},{2,3},{3,4},{4,5},{5,6},{6,7},{8,9},{9,10},{10,11},{11... | collective-permute-start | bytes 1572872 | tf_op jit(solution)/shard_map/ppermute | solution.py:47
  383.3 10.7 %collective-permute-start.18 = (bf16[512,512]{1,0:T(8,128)(2,1)}, bf16[512,512]{1,0:T(8,128)(2,1)S(1)}, u32[]{:S(2)}, u32[]{:S(2)}) collective-permute-start(bf16[512,512]{1,0:T(8,128)(2,1)} %fusion.983), channel_id=1, source_target_pairs={{0,1},{1,2},{2,3},{3,4},{4,5},{5,6},{6,7},{8,9},{9,10},{10,11},{11... | collective-permute-start | bytes 1572872 | tf_op jit(solution)/shard_map/ppermute | solution.py:47
  404.0 10.7 %collective-permute-start.19 = (bf16[512,512]{1,0:T(8,128)(2,1)}, bf16[512,512]{1,0:T(8,128)(2,1)S(1)}, u32[]{:S(2)}, u32[]{:S(2)}) collective-permute-start(bf16[512,512]{1,0:T(8,128)(2,1)} %fusion.980), channel_id=1, source_target_pairs={{0,1},{1,2},{2,3},{3,4},{4,5},{5,6},{6,7},{8,9},{9,10},{10,11},{11... | collective-permute-start | bytes 1572872 | tf_op jit(solution)/shard_map/ppermute | solution.py:47
  424.7 10.6 %collective-permute-start.20 = (bf16[512,512]{1,0:T(8,128)(2,1)}, bf16[512,512]{1,0:T(8,128)(2,1)S(1)}, u32[]{:S(2)}, u32[]{:S(2)}) collective-permute-start(bf16[512,512]{1,0:T(8,128)(2,1)} %fusion.977), channel_id=1, source_target_pairs={{0,1},{1,2},{2,3},{3,4},{4,5},{5,6},{6,7},{8,9},{9,10},{10,11},{11... | collective-permute-start | bytes 1572872 | tf_op jit(solution)/shard_map/ppermute | solution.py:47
  445.4 10.6 %collective-permute-start.21 = (bf16[512,512]{1,0:T(8,128)(2,1)}, bf16[512,512]{1,0:T(8,128)(2,1)S(1)}, u32[]{:S(2)}, u32[]{:S(2)}) collective-permute-start(bf16[512,512]{1,0:T(8,128)(2,1)} %fusion.974), channel_id=1, source_target_pairs={{0,1},{1,2},{2,3},{3,4},{4,5},{5,6},{6,7},{8,9},{9,10},{10,11},{11... | collective-permute-start | bytes 1572872 | tf_op jit(solution)/shard_map/ppermute | solution.py:47
  474.3 11.3 %collective-permute-start.22 = (bf16[512,512]{1,0:T(8,128)(2,1)S(1)}, bf16[512,512]{1,0:T(8,128)(2,1)S(1)}, u32[]{:S(2)}, u32[]{:S(2)}) collective-permute-start(bf16[512,512]{1,0:T(8,128)(2,1)S(1)} %fusion.1306), channel_id=1, source_target_pairs={{1,0},{2,1},{3,2},{4,3},{5,4},{6,5},{7,6},{9,8},{10,9},{11,10},{12... | collective-permute-start | bytes 1572872 | tf_op jit(solution)/shard_map/ppermute | solution.py:57
  494.4 10.5 %collective-permute-start.23 = (bf16[512,512]{1,0:T(8,128)(2,1)S(1)}, bf16[512,512]{1,0:T(8,128)(2,1)S(1)}, u32[]{:S(2)}, u32[]{:S(2)}) collective-permute-start(bf16[512,512]{1,0:T(8,128)(2,1)S(1)} %fusion.1305), channel_id=1, source_target_pairs={{1,0},{2,1},{3,2},{4,3},{5,4},{6,5},{7,6},{9,8},{10,9},{11,10},{12... | collective-permute-start | bytes 1572872 | tf_op jit(solution)/shard_map/ppermute | solution.py:57
  518.7 10.5 %collective-permute-start.24 = (bf16[512,512]{1,0:T(8,128)(2,1)S(1)}, bf16[512,512]{1,0:T(8,128)(2,1)S(1)}, u32[]{:S(2)}, u32[]{:S(2)}) collective-permute-start(bf16[512,512]{1,0:T(8,128)(2,1)S(1)} %fusion.1304), channel_id=1, source_target_pairs={{1,0},{2,1},{3,2},{4,3},{5,4},{6,5},{7,6},{9,8},{10,9},{11,10},{12... | collective-permute-start | bytes 1572872 | tf_op jit(solution)/shard_map/ppermute | solution.py:57
  543.1 10.5 %collective-permute-start.25 = (bf16[512,512]{1,0:T(8,128)(2,1)S(1)}, bf16[512,512]{1,0:T(8,128)(2,1)S(1)}, u32[]{:S(2)}, u32[]{:S(2)}) collective-permute-start(bf16[512,512]{1,0:T(8,128)(2,1)S(1)} %fusion.1303), channel_id=1, source_target_pairs={{1,0},{2,1},{3,2},{4,3},{5,4},{6,5},{7,6},{9,8},{10,9},{11,10},{12... | collective-permute-start | bytes 1572872 | tf_op jit(solution)/shard_map/ppermute | solution.py:57
  567.5 10.5 %collective-permute-start.26 = (bf16[512,512]{1,0:T(8,128)(2,1)S(1)}, bf16[512,512]{1,0:T(8,128)(2,1)S(1)}, u32[]{:S(2)}, u32[]{:S(2)}) collective-permute-start(bf16[512,512]{1,0:T(8,128)(2,1)S(1)} %fusion.1302), channel_id=1, source_target_pairs={{1,0},{2,1},{3,2},{4,3},{5,4},{6,5},{7,6},{9,8},{10,9},{11,10},{12... | collective-permute-start | bytes 1572872 | tf_op jit(solution)/shard_map/ppermute | solution.py:57
  592.0 10.5 %collective-permute-start.27 = (bf16[512,512]{1,0:T(8,128)(2,1)S(1)}, bf16[512,512]{1,0:T(8,128)(2,1)S(1)}, u32[]{:S(2)}, u32[]{:S(2)}) collective-permute-start(bf16[512,512]{1,0:T(8,128)(2,1)S(1)} %fusion.1301), channel_id=1, source_target_pairs={{1,0},{2,1},{3,2},{4,3},{5,4},{6,5},{7,6},{9,8},{10,9},{11,10},{12... | collective-permute-start | bytes 1572872 | tf_op jit(solution)/shard_map/ppermute | solution.py:57
  616.4 10.5 %collective-permute-start.28 = (bf16[512,512]{1,0:T(8,128)(2,1)S(1)}, bf16[512,512]{1,0:T(8,128)(2,1)S(1)}, u32[]{:S(2)}, u32[]{:S(2)}) collective-permute-start(bf16[512,512]{1,0:T(8,128)(2,1)S(1)} %fusion.1300), channel_id=1, source_target_pairs={{1,0},{2,1},{3,2},{4,3},{5,4},{6,5},{7,6},{9,8},{10,9},{11,10},{12... | collective-permute-start | bytes 1572872 | tf_op jit(solution)/shard_map/ppermute | solution.py:57
  640.8 10.5 %collective-permute-start.29 = (bf16[512,512]{1,0:T(8,128)(2,1)S(1)}, bf16[512,512]{1,0:T(8,128)(2,1)S(1)}, u32[]{:S(2)}, u32[]{:S(2)}) collective-permute-start(bf16[512,512]{1,0:T(8,128)(2,1)S(1)} %fusion.1299), channel_id=1, source_target_pairs={{1,0},{2,1},{3,2},{4,3},{5,4},{6,5},{7,6},{9,8},{10,9},{11,10},{12... | collective-permute-start | bytes 1572872 | tf_op jit(solution)/shard_map/ppermute | solution.py:57
  665.3 10.5 %collective-permute-start.30 = (bf16[512,512]{1,0:T(8,128)(2,1)S(1)}, bf16[512,512]{1,0:T(8,128)(2,1)S(1)}, u32[]{:S(2)}, u32[]{:S(2)}) collective-permute-start(bf16[512,512]{1,0:T(8,128)(2,1)S(1)} %fusion.1298), channel_id=1, source_target_pairs={{1,0},{2,1},{3,2},{4,3},{5,4},{6,5},{7,6},{9,8},{10,9},{11,10},{12... | collective-permute-start | bytes 1572872 | tf_op jit(solution)/shard_map/ppermute | solution.py:57
  689.7 10.5 %collective-permute-start.31 = (bf16[512,512]{1,0:T(8,128)(2,1)S(1)}, bf16[512,512]{1,0:T(8,128)(2,1)S(1)}, u32[]{:S(2)}, u32[]{:S(2)}) collective-permute-start(bf16[512,512]{1,0:T(8,128)(2,1)S(1)} %fusion.1297), channel_id=1, source_target_pairs={{1,0},{2,1},{3,2},{4,3},{5,4},{6,5},{7,6},{9,8},{10,9},{11,10},{12... | collective-permute-start | bytes 1572872 | tf_op jit(solution)/shard_map/ppermute | solution.py:57
  787.4 10.5 %collective-permute-start.35 = (bf16[512,512]{1,0:T(8,128)(2,1)S(1)}, bf16[512,512]{1,0:T(8,128)(2,1)S(1)}, u32[]{:S(2)}, u32[]{:S(2)}) collective-permute-start(bf16[512,512]{1,0:T(8,128)(2,1)S(1)} %fusion.1293), channel_id=1, source_target_pairs={{1,0},{2,1},{3,2},{4,3},{5,4},{6,5},{7,6},{9,8},{10,9},{11,10},{12... | collective-permute-start | bytes 1572872 | tf_op jit(solution)/shard_map/ppermute | solution.py:57
  885.3 10.5 %collective-permute-start.39 = (bf16[512,512]{1,0:T(8,128)(2,1)S(1)}, bf16[512,512]{1,0:T(8,128)(2,1)S(1)}, u32[]{:S(2)}, u32[]{:S(2)}) collective-permute-start(bf16[512,512]{1,0:T(8,128)(2,1)S(1)} %fusion.1289), channel_id=1, source_target_pairs={{1,0},{2,1},{3,2},{4,3},{5,4},{6,5},{7,6},{9,8},{10,9},{11,10},{12... | collective-permute-start | bytes 1572872 | tf_op jit(solution)/shard_map/ppermute | solution.py:57
  958.6 10.5 %collective-permute-start.42 = (bf16[512,512]{1,0:T(8,128)(2,1)S(1)}, bf16[512,512]{1,0:T(8,128)(2,1)S(1)}, u32[]{:S(2)}, u32[]{:S(2)}) collective-permute-start(bf16[512,512]{1,0:T(8,128)(2,1)S(1)} %fusion.1286), channel_id=1, source_target_pairs={{1,0},{2,1},{3,2},{4,3},{5,4},{6,5},{7,6},{9,8},{10,9},{11,10},{12... | collective-permute-start | bytes 1572872 | tf_op jit(solution)/shard_map/ppermute | solution.py:57
  (70 other events, 456.7 us)
where the time goes:
time: 1050 us; the launch traced here: 1030 us
  matrix products  584 us (56%)
  waiting for transfers between devices  148 us (14%)
  starting transfers between devices  147 us (14%)
  other arithmetic  97.6 us (9%)
  local copies, waits for them, and re-layouts  50.8 us (5%)
    dot_general x68, matrix products, matmul(): jnp.dot(a, w, preferred_element_type=jnp.float32).astype(jnp.bfloat16)  228 us
    dot_general x90, matrix products, layer(): gate = jnp.dot(a, w['w_gate'], preferred_element_type=jnp.float32)  197 us
    dot_general x68, matrix products, layer(): up = jnp.dot(a, w['w_up'], preferred_element_type=jnp.float32)  159 us
    ppermute x22, starting transfers between devices, step(): came = lax.ppermute(stage(weights, h), 'pp', onward)  97.7 us
    ppermute x22, waiting for transfers between devices, step(): came = lax.ppermute(by_h, 'pp', back_again)  84.5 us
    ppermute x22, waiting for transfers between devices, step(): came = lax.ppermute(stage(weights, h), 'pp', onward)  63.2 us
    ppermute x22, starting transfers between devices, step(): came = lax.ppermute(by_h, 'pp', back_again)  48.9 us
    dynamic_update_slice x23, other arithmetic, step(): lax.dynamic_update_index_in_dim(kept, jnp.where(at_work, h, was), number, 0)  35.3 us
  transfers between devices with their start and end apart: 44, of which 41 were waited for; matrix products, arithmetic and copies ran while one was open for 17% of the time, Pallas kernels for 0%

commit v1 on v0

v1 whole, which is shorter than its diff:
```python
import functools

import jax
import jax.numpy as jnp
from jax import lax
from jax.experimental import pallas as pl
from jax.experimental.pallas import tpu as pltpu
from jax.sharding import PartitionSpec as P

MESH = pl.DeviceIdType.MESH
F32, BF16 = jnp.float32, jnp.bfloat16
BLOCKS = 2
LANES = 128
AHEAD = 2
LAG = 2
SENDS = 4
EPS = 1e-6


def dot(a, b):
    return jnp.dot(a, b, preferred_element_type=F32)


def kernel(
    stages, micro, blocks,
    x_ref, dy_ref, wg_ref, wu_ref, wd_ref, dgu_out, dwd_out,
    wgu, wd, wgu_t, wd_t, hs, norms, grads, fsend, bsend, act_tmp, acts, dgus, turned, acc_gu, acc_d,
    w_sem, wd_sem, out_sem, recv_f, recv_b, send_f, send_b,
):
    me = lax.axis_index("pp")
    rows, d = hs.shape[1:]
    ff = wd.shape[0]
    first, last = me == 0, me == stages - 1
    pieces = ff // LANES
    wide = [(c, min(2 * LANES, ff - c)) for c in range(0, ff, 2 * LANES)]

    for c in range(pieces):
        at = pl.ds(c * LANES, LANES)
        pltpu.make_async_copy(wg_ref.at[0, :, at], wgu.at[:, pl.ds(2 * c * LANES, LANES)], w_sem).start()
        pltpu.make_async_copy(wu_ref.at[0, :, at], wgu.at[:, pl.ds((2 * c + 1) * LANES, LANES)], w_sem).start()
    pltpu.make_async_copy(wd_ref.at[0], wd, wd_sem).start()

    def x_copy(b):
        return pltpu.make_async_copy(x_ref.at[b], hs.at[b], recv_f.at[b])

    def dy_copy(b):
        return pltpu.make_async_copy(dy_ref.at[b], grads.at[b], recv_b.at[b])

    def f_copy(b):
        slot = lax.rem(b, SENDS)
        return pltpu.make_async_remote_copy(
            src_ref=fsend.at[slot], dst_ref=hs.at[b], send_sem=send_f.at[slot], recv_sem=recv_f.at[b],
            device_id={"pp": me + 1}, device_id_type=MESH,
        )

    def b_copy(b):
        slot = lax.rem(b, SENDS)
        return pltpu.make_async_remote_copy(
            src_ref=bsend.at[slot], dst_ref=grads.at[b], send_sem=send_b.at[slot], recv_sem=recv_b.at[b],
            device_id={"pp": me - 1}, device_id_type=MESH,
        )

    barrier = pltpu.get_barrier_semaphore()

    @pl.when(me > 0)
    def _():
        pl.semaphore_signal(barrier, inc=1, device_id={"pp": me - 1}, device_id_type=MESH)

    @pl.when(me < stages - 1)
    def _():
        pl.semaphore_signal(barrier, inc=1, device_id={"pp": me + 1}, device_id_type=MESH)

    total_blocks = micro * blocks

    @pl.when(first)
    def _():
        @pl.loop(0, total_blocks)
        def _(b):
            x_copy(b).start()

    @pl.when(last)
    def _():
        @pl.loop(0, total_blocks)
        def _(b):
            dy_copy(b).start()

    acc_gu[...] = jnp.zeros_like(acc_gu)
    acc_d[...] = jnp.zeros_like(acc_d)
    pltpu.make_async_copy(wgu, wgu, w_sem).wait()
    pltpu.make_async_copy(wd_ref.at[0], wd, wd_sem).wait()

    def turn_weights():
        for c in range(pieces):
            at = pl.ds(c * LANES, LANES)
            wd_t[:, at] = wd[at, :].T
        for c in range(2 * pieces):
            at = pl.ds(c * LANES, LANES)
            wgu_t[at, :] = wgu[:, at].T

    @pl.when(me > 0)
    def _():
        turn_weights()

    pl.semaphore_wait(barrier, jnp.where(first | last, 1, 2))

    def gated(gu, n):
        g = jnp.concatenate([gu[:, 2 * i * LANES:(2 * i + 1) * LANES] for i in range(n)], axis=1)
        u = jnp.concatenate([gu[:, (2 * i + 1) * LANES:(2 * i + 2) * LANES] for i in range(n)], axis=1)
        return g, u, 0.5 * jnp.tanh(0.5 * g) + 0.5

    def forward(b):
        @pl.when(first)
        def _():
            x_copy(b).wait()

        @pl.when(me > 0)
        def _():
            f_copy(b).wait_recv()

        h = hs[b].astype(F32)
        scale = lax.rsqrt(jnp.mean(h * h, -1, keepdims=True) + EPS)
        a = (h * scale).astype(BF16)
        norms[b] = a

        @pl.when(me < stages - 1)
        def _():
            @pl.when(b >= SENDS)
            def _():
                f_copy(b - SENDS).wait_send()

            for c, w in wide:
                gu = dot(norms[b], wgu[:, 2 * c:2 * c + 2 * w])
                g, u, s = gated(gu, w // LANES)
                act_tmp[:, c:c + w] = (g * s * u).astype(BF16)
            y = dot(act_tmp[...], wd[...]).astype(BF16)
            fsend[lax.rem(b, SENDS)] = (hs[b].astype(F32) + y.astype(F32)).astype(BF16)
            f_copy(b).start()

    def backward(b, ring):
        @pl.when(last)
        def _():
            dy_copy(b).wait()

        @pl.when(me < stages - 1)
        def _():
            pltpu.make_async_remote_copy(
                src_ref=bsend.at[0], dst_ref=grads.at[b], send_sem=send_b.at[0], recv_sem=recv_b.at[b],
                device_id={"pp": me + 1}, device_id_type=MESH,
            ).wait_recv()

        part = lax.rem(b, blocks)
        slot = ring * blocks + part
        for c, w in wide:
            gu = dot(norms[b], wgu[:, 2 * c:2 * c + 2 * w])
            dact = dot(grads[b], wd_t[:, c:c + w]).astype(BF16).astype(F32)
            g, u, s = gated(gu, w // LANES)
            silu = g * s
            acts[slot, :, c:c + w] = (silu * u).astype(BF16)
            dup = dact * silu
            dgate = dact * u * (s + silu * (1.0 - s))
            both = []
            for i in range(w // LANES):
                both += [dgate[:, i * LANES:(i + 1) * LANES], dup[:, i * LANES:(i + 1) * LANES]]
            dgus[slot, :, 2 * c:2 * c + 2 * w] = jnp.concatenate(both, axis=1).astype(BF16)

        @pl.when(me > 0)
        def _():
            @pl.when(b >= SENDS)
            def _():
                b_copy(b - SENDS).wait_send()

            da = dot(dgus[slot], wgu_t[...]).astype(BF16).astype(F32)
            h = hs[b].astype(F32)
            scale = lax.rsqrt(jnp.mean(h * h, -1, keepdims=True) + EPS)
            pull = jnp.mean(da * h, -1, keepdims=True) * (scale * scale * scale)
            dh = (da * scale - h * pull).astype(BF16).astype(F32)
            bsend[lax.rem(b, SENDS)] = (grads[b].astype(F32) + dh).astype(BF16)
            b_copy(b).start()

    tokens = rows * blocks

    def whole(ref, start, cols):
        return ref[pl.ds(start, blocks), :, cols].reshape(tokens, -1)

    def weight(k, ring):
        turned[0] = whole(norms, k * blocks, slice(None)).T
        turned[1] = whole(grads, k * blocks, slice(None)).T
        base = ring * blocks
        for c in range(0, 2 * ff, 2 * LANES):
            term = dot(turned[0], whole(dgus, base, slice(c, c + 2 * LANES)))
            acc_gu[:, c:c + 2 * LANES] += term.astype(BF16).astype(F32)
        for c, w in wide:
            term = dot(turned[1], whole(acts, base, slice(c, c + w)))
            acc_d[:, c:c + w] += term.astype(BF16).astype(F32)

    ahead = AHEAD * (stages - 1 - me)
    ahead = jnp.minimum(ahead, micro)

    @pl.loop(0, micro + min(AHEAD * (stages - 1), micro) + LAG)
    def _(t):
        @pl.when(first & (t == micro // 2))
        def _():
            turn_weights()

        @pl.when(t < micro)
        def _():
            @pl.loop(0, blocks)
            def _(j):
                forward(t * blocks + j)

        kb = t - ahead

        @pl.when((kb >= 0) & (kb < micro))
        def _():
            @pl.loop(0, blocks)
            def _(j):
                backward(kb * blocks + j, lax.rem(kb, LAG + 1))

        kw = kb - LAG

        @pl.when((kw >= 0) & (kw < micro))
        def _():
            weight(kw, lax.rem(kw, LAG + 1))

    copies = []
    for j in range(blocks):
        at = pl.ds(j * rows, rows)
        dgus[j] = acc_gu[j * rows:(j + 1) * rows, :].astype(BF16)
        acts[j] = acc_d[j * rows:(j + 1) * rows, :].astype(BF16)
        copies.append(pltpu.make_async_copy(dgus.at[j], dgu_out.at[at], out_sem.at[2 * j]))
        copies.append(pltpu.make_async_copy(acts.at[j], dwd_out.at[at], out_sem.at[2 * j + 1]))
        copies[-2].start()
        copies[-1].start()

    @pl.when(me < stages - 1)
    def _():
        @pl.loop(total_blocks - SENDS, total_blocks)
        def _(b):
            f_copy(b).wait_send()

    @pl.when(me > 0)
    def _():
        @pl.loop(total_blocks - SENDS, total_blocks)
        def _(b):
            b_copy(b).wait_send()

    for copy in copies:
        copy.wait()


def solution(mesh):
    stages = mesh.shape["pp"]

    def step(x, dy, w_gate, w_up, w_down):
        micro, tokens, d = x.shape
        ff = w_gate.shape[-1]
        rows = tokens // BLOCKS
        count = micro * BLOCKS
        ring = (LAG + 1) * BLOCKS
        any_space = pl.BlockSpec(memory_space=pl.ANY)
        dgu, dwd = pl.pallas_call(
            functools.partial(kernel, stages, micro, BLOCKS),
            out_shape=(jax.ShapeDtypeStruct((d, 2 * ff), BF16), jax.ShapeDtypeStruct((d, ff), BF16)),
            in_specs=[any_space] * 5,
            out_specs=(any_space,) * 2,
            scratch_shapes=[
                pltpu.VMEM((d, 2 * ff), BF16),
                pltpu.VMEM((ff, d), BF16),
                pltpu.VMEM((2 * ff, d), BF16),
                pltpu.VMEM((d, ff), BF16),
                pltpu.VMEM((count, rows, d), BF16),
                pltpu.VMEM((count, rows, d), BF16),
                pltpu.VMEM((count, rows, d), BF16),
                pltpu.VMEM((SENDS, rows, d), BF16),
                pltpu.VMEM((SENDS, rows, d), BF16),
                pltpu.VMEM((rows, ff), BF16),
                pltpu.VMEM((ring, rows, ff), BF16),
                pltpu.VMEM((ring, rows, 2 * ff), BF16),
                pltpu.VMEM((2, d, tokens), BF16),
                pltpu.VMEM((d, 2 * ff), F32),
                pltpu.VMEM((d, ff), F32),
                pltpu.SemaphoreType.DMA,
                pltpu.SemaphoreType.DMA,
                pltpu.SemaphoreType.DMA((2 * BLOCKS,)),
                pltpu.SemaphoreType.DMA((count,)),
                pltpu.SemaphoreType.DMA((count,)),
                pltpu.SemaphoreType.DMA((SENDS,)),
                pltpu.SemaphoreType.DMA((SENDS,)),
            ],
            compiler_params=pltpu.CompilerParams(collective_id=0, has_side_effects=True, vmem_limit_bytes=67_043_328),
            name="stage",
        )(x.reshape(count, rows, d), dy.reshape(count, rows, d), w_gate, w_up, w_down)
        pairs = dgu.reshape(d, ff // LANES, 2, LANES)
        return pairs[:, :, 0].reshape(1, d, ff), pairs[:, :, 1].reshape(1, d, ff), dwd.T[None]

    return jax.shard_map(
        step,
        mesh=mesh,
        in_specs=(P("rep", None, None),) * 2 + (P("pp", None, None),) * 3,
        out_specs=(P(("rep", "pp"), None, None),) * 3,
        check_vma=False,
    )
```

time: 1050 us -> 272 us (0.26)
  the two profiles are of different devices: /device:TPU:113 before, /device:TPU:120 now
where the time goes in v1:
time: 272 us; the launch traced here: 271 us
  Pallas kernels  239 us (88%)
  local copies, waits for them, and re-layouts  32.1 us (12%)
    pallas_call x1, Pallas kernels, step(): pl.pallas_call(functools.partial(kernel, stages, micro, BLOCKS), out_shap...  239 us
    unnamed x7, local copies, waits for them, and re-layouts  21.1 us
    slice x1, local copies, waits for them, and re-layouts, step(): pairs[:, :, 1].reshape(1, d, ff)  5.6 us

profile of v1, /device:TPU:120, one launch (start us, length us, event | category | flops | bytes accessed | tf_op | source)
XLA Modules:
  0.0 271.4 jit_solution(2461546995033742777)
XLA Ops:
  0.6 238.6 %stage.1 = (bf16[512,2816]{1,0:T(8,128)(2,1)}, bf16[512,1408]{1,0:T(8,128)(2,1)}) custom-call(bf16[32,256,512]{2,1,0:T(8,128)(2,1)} %bitcast.7, bf16[32,256,512]{2,1,0:T(8,128)(2,1)} %bitcast.8, bf16[1,512,1408]{2,1,0:T(8,128)(2,1)} %wg_ref.1, bf16[1,512,1408]{2,1,0:T(8,128)(2,1)} %wu_ref.1, bf16[1,1408,512]{2,1,0:T(8,128)(2,1)} %wd_ref.1), custom_call_target="tpu_custom_call" | custom-call | tf_op jit(solution)/shard_map/stage/pallas_call | solution.py:261
  239.3 5.3 %reshape.17 = bf16[512,11,2,128]{3,2,1,0:T(2,128)(2,1)S(1)} reshape(bf16[512,2816]{1,0:T(8,128)(2,1)} %get-tuple-element.5) | data formatting | bytes 5767168 | tf_op jit(solution)/shard_map/reshape | solution.py:293
  244.6 2.5 copy.13
  247.2 5.6 %fusion = (bf16[512,11,1,128]{3,2,1,0:T(2,128)(2,1)}, bf16[512,11,1,128]{3,2,1,0:T(2,128)(2,1)}) fusion(bf16[512,11,2,128]{3,2,1,0:T(2,128)(2,1)S(1)} %reshape.17), kind=kLoop, calls=%fused_computation | loop fusion | bytes 5767168 | tf_op jit(solution)/shard_map/slice | solution.py:294
  252.8 0.0 copy-start
  252.8 7.7 %copy.15 = bf16[512,11,1,128]{0,3,1,2:T(8,128)(2,1)} copy(bf16[512,11,1,128]{3,2,1,0:T(2,128)(2,1)} %get-tuple-element.13) | data formatting | bytes 2883584
  260.5 2.5 copy.12
  263.0 0.0 copy-done
  263.0 5.8 %copy.14 = bf16[512,11,1,128]{0,3,1,2:T(8,128)(2,1)} copy(bf16[512,11,1,128]{3,2,1,0:T(2,128)(2,1)S(1)} %copy-done) | data formatting | bytes 2883584
  268.8 2.5 copy.11
Async XLA Ops:
  252.8 10.3 %copy-start = (bf16[512,11,1,128]{3,2,1,0:T(2,128)(2,1)S(1)}, bf16[512,11,1,128]{3,2,1,0:T(2,128)(2,1)}, u32[]{:S(2)}) copy-start(bf16[512,11,1,128]{3,2,1,0:T(2,128)(2,1)} %get-tuple-element.14) | copy-start | bytes 4325380

commit v2 on v1

v2 whole, which is shorter than its diff:
```python
import functools

import jax
import jax.numpy as jnp
from jax import lax
from jax.experimental import pallas as pl
from jax.experimental.pallas import tpu as pltpu
from jax.sharding import PartitionSpec as P

MESH = pl.DeviceIdType.MESH
F32, BF16 = jnp.float32, jnp.bfloat16
BLOCKS = 2
LANES = 128
AHEAD = 2
LAG = 0
SENDS = 4
EPS = 1e-6


def dot(a, b):
    return jnp.dot(a, b, preferred_element_type=F32)


def kernel(
    stages, micro, blocks,
    x_ref, dy_ref, wg_ref, wu_ref, wd_ref, out_g, out_u, out_d, slopes_hbm, acts_hbm,
    wgu, wd, wgu_t, wd_t, hs, norms, grads, fsend, bsend, slopes, acts, dgus, turned, acc_gu, acc_d,
    w_sem, wd_sem, out_sem, recv_f, recv_b, send_f, send_b, put_s, put_a, get_s, get_a,
):
    me = lax.axis_index("pp")
    rows, d = hs.shape[1:]
    ff = wd.shape[0]
    first, last = me == 0, me == stages - 1
    pieces = ff // LANES
    wide = [(c, min(2 * LANES, ff - c)) for c in range(0, ff, 2 * LANES)]
    total_blocks = micro * blocks
    ring = (LAG + 1) * blocks

    def x_copy(b):
        return pltpu.make_async_copy(x_ref.at[b], hs.at[b], recv_f.at[b])

    def dy_copy(b):
        return pltpu.make_async_copy(dy_ref.at[b], grads.at[b], recv_b.at[b])

    def f_copy(b):
        slot = lax.rem(b, SENDS)
        return pltpu.make_async_remote_copy(
            src_ref=fsend.at[slot], dst_ref=hs.at[b], send_sem=send_f.at[slot], recv_sem=recv_f.at[b],
            device_id={"pp": me + 1}, device_id_type=MESH,
        )

    def b_copy(b):
        slot = lax.rem(b, SENDS)
        return pltpu.make_async_remote_copy(
            src_ref=bsend.at[slot], dst_ref=grads.at[b], send_sem=send_b.at[slot], recv_sem=recv_b.at[b],
            device_id={"pp": me - 1}, device_id_type=MESH,
        )

    def put_slopes(b):
        slot = lax.rem(b, 2)
        return pltpu.make_async_copy(slopes.at[2 + slot], slopes_hbm.at[b], put_s.at[slot])

    def put_acts(b):
        slot = lax.rem(b, 2)
        return pltpu.make_async_copy(acts.at[ring + slot], acts_hbm.at[b], put_a.at[slot])

    def get_slopes(b):
        slot = lax.rem(b, 2)
        return pltpu.make_async_copy(slopes_hbm.at[b], slopes.at[slot], get_s.at[slot])

    def get_acts(b):
        slot = lax.rem(b, ring)
        return pltpu.make_async_copy(acts_hbm.at[b], acts.at[slot], get_a.at[slot])

    @pl.when(first)
    def _():
        x_copy(0).start()

    for c in range(pieces):
        at = pl.ds(c * LANES, LANES)
        pltpu.make_async_copy(wg_ref.at[0, :, at], wgu.at[:, pl.ds(2 * c * LANES, LANES)], w_sem).start()
        pltpu.make_async_copy(wu_ref.at[0, :, at], wgu.at[:, pl.ds((2 * c + 1) * LANES, LANES)], w_sem).start()
    pltpu.make_async_copy(wd_ref.at[0], wd, wd_sem).start()

    barrier = pltpu.get_barrier_semaphore()

    @pl.when(me > 0)
    def _():
        pl.semaphore_signal(barrier, inc=1, device_id={"pp": me - 1}, device_id_type=MESH)

    @pl.when(me < stages - 1)
    def _():
        pl.semaphore_signal(barrier, inc=1, device_id={"pp": me + 1}, device_id_type=MESH)

    @pl.when(first)
    def _():
        @pl.loop(1, total_blocks)
        def _(b):
            x_copy(b).start()

    @pl.when(last)
    def _():
        @pl.loop(0, total_blocks)
        def _(b):
            dy_copy(b).start()

    pltpu.make_async_copy(wgu, wgu, w_sem).wait()
    pltpu.make_async_copy(wd_ref.at[0], wd, wd_sem).wait()

    def turn_weights():
        acc_gu[...] = jnp.zeros_like(acc_gu)
        acc_d[...] = jnp.zeros_like(acc_d)
        for c in range(pieces):
            at = pl.ds(c * LANES, LANES)
            wd_t[:, at] = wd[at, :].T
        for c in range(2 * pieces):
            at = pl.ds(c * LANES, LANES)
            wgu_t[at, :] = wgu[:, at].T

    @pl.when(me > 0)
    def _():
        turn_weights()

    pl.semaphore_wait(barrier, jnp.where(first | last, 1, 2))

    def gated(gu, n):
        g = jnp.concatenate([gu[:, 2 * i * LANES:(2 * i + 1) * LANES] for i in range(n)], axis=1)
        u = jnp.concatenate([gu[:, (2 * i + 1) * LANES:(2 * i + 2) * LANES] for i in range(n)], axis=1)
        return g, u, 0.5 * jnp.tanh(0.5 * g) + 0.5

    def forward(b):
        @pl.when(first)
        def _():
            x_copy(b).wait()

        @pl.when(me > 0)
        def _():
            f_copy(b).wait_recv()

        h = hs[b].astype(F32)
        scale = lax.rsqrt(jnp.mean(h * h, -1, keepdims=True) + EPS)
        a = (h * scale).astype(BF16)
        norms[b] = a

        @pl.when((me < stages - 1) & (b >= 2))
        def _():
            put_slopes(b - 2).wait()
            put_acts(b - 2).wait()

        to_s = jnp.where(last, lax.rem(b, 2), 2 + lax.rem(b, 2))
        to_a = jnp.where(last, lax.rem(b, ring), ring + lax.rem(b, 2))
        for c, w in wide:
            gu = dot(norms[b], wgu[:, 2 * c:2 * c + 2 * w])
            g, u, s = gated(gu, w // LANES)
            silu = g * s
            slopes[to_s, :, c:c + w] = silu
            slopes[to_s, :, ff + c:ff + c + w] = u * (s + silu * (1.0 - s))
            acts[to_a, :, c:c + w] = (silu * u).astype(BF16)

        @pl.when(me < stages - 1)
        def _():
            put_slopes(b).start()
            put_acts(b).start()

            @pl.when(b >= SENDS)
            def _():
                f_copy(b - SENDS).wait_send()

            y = dot(acts[to_a], wd[...]).astype(BF16)
            fsend[lax.rem(b, SENDS)] = (hs[b].astype(F32) + y.astype(F32)).astype(BF16)
            f_copy(b).start()

    def backward(b):
        @pl.when(last)
        def _():
            dy_copy(b).wait()

        @pl.when(me < stages - 1)
        def _():
            get_acts(b).start()

            @pl.when(b + 1 < total_blocks)
            def _():
                get_slopes(b + 1).start()

            pltpu.make_async_remote_copy(
                src_ref=bsend.at[0], dst_ref=grads.at[b], send_sem=send_b.at[0], recv_sem=recv_b.at[b],
                device_id={"pp": me + 1}, device_id_type=MESH,
            ).wait_recv()
            get_slopes(b).wait()

        at_s, slot = lax.rem(b, 2), lax.rem(b, ring)
        for c, w in wide:
            dact = dot(grads[b], wd_t[:, c:c + w]).astype(BF16).astype(F32)
            dgate = (dact * slopes[at_s, :, ff + c:ff + c + w]).astype(BF16)
            dup = (dact * slopes[at_s, :, c:c + w]).astype(BF16)
            for i in range(w // LANES):
                at = 2 * c + 2 * i * LANES
                dgus[slot, :, at:at + LANES] = dgate[:, i * LANES:(i + 1) * LANES]
                dgus[slot, :, at + LANES:at + 2 * LANES] = dup[:, i * LANES:(i + 1) * LANES]

        @pl.when(me > 0)
        def _():
            @pl.when(b >= SENDS)
            def _():
                b_copy(b - SENDS).wait_send()

            da = dot(dgus[slot], wgu_t[...]).astype(BF16).astype(F32)
            h = hs[b].astype(F32)
            scale = lax.rsqrt(jnp.mean(h * h, -1, keepdims=True) + EPS)
            pull = jnp.mean(da * h, -1, keepdims=True) * (scale * scale * scale)
            dh = (da * scale - h * pull).astype(BF16).astype(F32)
            bsend[lax.rem(b, SENDS)] = (grads[b].astype(F32) + dh).astype(BF16)
            b_copy(b).start()

    tokens = rows * blocks

    def whole(ref, start, cols):
        return ref[pl.ds(start, blocks), :, cols].reshape(tokens, -1)

    def weight(k):
        base = lax.rem(k, LAG + 1) * blocks

        @pl.when(me < stages - 1)
        def _():
            @pl.loop(0, blocks)
            def _(j):
                get_acts(k * blocks + j).wait()

        turned[0] = whole(norms, k * blocks, slice(None)).T
        turned[1] = whole(grads, k * blocks, slice(None)).T
        for c in range(0, 2 * ff, 2 * LANES):
            term = dot(turned[0], whole(dgus, base, slice(c, c + 2 * LANES)))
            acc_gu[:, c:c + 2 * LANES] += term.astype(BF16).astype(F32)
        for c, w in wide:
            term = dot(turned[1], whole(acts, base, slice(c, c + w)))
            acc_d[:, c:c + w] += term.astype(BF16).astype(F32)

    ahead = jnp.minimum(AHEAD * (stages - 1 - me), micro)

    @pl.loop(0, micro + min(AHEAD * (stages - 1), micro) + LAG)
    def _(t):
        kb = t - ahead
        kw = kb - LAG

        @pl.when(first & (t == 1))
        def _():
            turn_weights()

        @pl.when((me < stages - 1) & (kb == 0))
        def _():
            get_slopes(0).start()

        @pl.when((me < stages - 1) & (t == micro))
        def _():
            for b in (total_blocks - 2, total_blocks - 1):
                put_slopes(b).wait()
                put_acts(b).wait()

        @pl.loop(0, blocks)
        def _(j):
            @pl.when(t < micro)
            def _():
                forward(t * blocks + j)

            @pl.when((kb >= 0) & (kb < micro))
            def _():
                backward(kb * blocks + j)

        @pl.when((kw >= 0) & (kw < micro))
        def _():
            weight(kw)

    copies = []

    def out(src, dst):
        copies.append(pltpu.make_async_copy(src, dst, out_sem.at[len(copies)]))
        copies[-1].start()

    for j in range(blocks):
        at = slice(j * rows, (j + 1) * rows)
        for c in range(pieces):
            dgus[j, :, c * LANES:(c + 1) * LANES] = acc_gu[at, 2 * c * LANES:(2 * c + 1) * LANES].astype(BF16)
            dgus[j, :, ff + c * LANES:ff + (c + 1) * LANES] = acc_gu[at, (2 * c + 1) * LANES:(2 * c + 2) * LANES].astype(BF16)
        out(dgus.at[j, :, pl.ds(0, ff)], out_g.at[0, pl.ds(j * rows, rows)])
        out(dgus.at[j, :, pl.ds(ff, ff)], out_u.at[0, pl.ds(j * rows, rows)])
    for c in range(pieces):
        at = slice(c * LANES, (c + 1) * LANES)
        wd[at, :] = acc_d[:, at].astype(BF16).T
    out(wd, out_d.at[0])

    @pl.when(me < stages - 1)
    def _():
        @pl.loop(total_blocks - SENDS, total_blocks)
        def _(b):
            f_copy(b).wait_send()

    @pl.when(me > 0)
    def _():
        @pl.loop(total_blocks - SENDS, total_blocks)
        def _(b):
            b_copy(b).wait_send()

    for copy in copies:
        copy.wait()


def solution(mesh):
    stages = mesh.shape["pp"]

    def step(x, dy, w_gate, w_up, w_down):
        micro, tokens, d = x.shape
        ff = w_gate.shape[-1]
        rows = tokens // BLOCKS
        count = micro * BLOCKS
        ring = (LAG + 1) * BLOCKS
        any_space = pl.BlockSpec(memory_space=pl.ANY)
        out_g, out_u, out_d, _, _ = pl.pallas_call(
            functools.partial(kernel, stages, micro, BLOCKS),
            out_shape=(
                jax.ShapeDtypeStruct((1, d, ff), BF16),
                jax.ShapeDtypeStruct((1, d, ff), BF16),
                jax.ShapeDtypeStruct((1, ff, d), BF16),
                jax.ShapeDtypeStruct((count, rows, 2 * ff), F32),
                jax.ShapeDtypeStruct((count, rows, ff), BF16),
            ),
            in_specs=[any_space] * 5,
            out_specs=(any_space,) * 5,
            scratch_shapes=[
                pltpu.VMEM((d, 2 * ff), BF16),
                pltpu.VMEM((ff, d), BF16),
                pltpu.VMEM((2 * ff, d), BF16),
                pltpu.VMEM((d, ff), BF16),
                pltpu.VMEM((count, rows, d), BF16),
                pltpu.VMEM((count, rows, d), BF16),
                pltpu.VMEM((count, rows, d), BF16),
                pltpu.VMEM((SENDS, rows, d), BF16),
                pltpu.VMEM((SENDS, rows, d), BF16),
                pltpu.VMEM((4, rows, 2 * ff), F32),
                pltpu.VMEM((ring + 2, rows, ff), BF16),
                pltpu.VMEM((ring, rows, 2 * ff), BF16),
                pltpu.VMEM((2, d, tokens), BF16),
                pltpu.VMEM((d, 2 * ff), F32),
                pltpu.VMEM((d, ff), F32),
                pltpu.SemaphoreType.DMA,
                pltpu.SemaphoreType.DMA,
                pltpu.SemaphoreType.DMA((2 * BLOCKS + 1,)),
                pltpu.SemaphoreType.DMA((count,)),
                pltpu.SemaphoreType.DMA((count,)),
                pltpu.SemaphoreType.DMA((SENDS,)),
                pltpu.SemaphoreType.DMA((SENDS,)),
                pltpu.SemaphoreType.DMA((2,)),
                pltpu.SemaphoreType.DMA((2,)),
                pltpu.SemaphoreType.DMA((2,)),
                pltpu.SemaphoreType.DMA((ring,)),
            ],
            compiler_params=pltpu.CompilerParams(collective_id=0, has_side_effects=True, vmem_limit_bytes=67_043_328),
            name="stage",
        )(x.reshape(count, rows, d), dy.reshape(count, rows, d), w_gate, w_up, w_down)
        return out_g, out_u, out_d

    return jax.shard_map(
        step,
        mesh=mesh,
        in_specs=(P("rep", None, None),) * 2 + (P("pp", None, None),) * 3,
        out_specs=(P(("rep", "pp"), None, None),) * 3,
        check_vma=False,
    )
```

time: 272 us -> 225 us (0.83)
  local copies, waits for them, and re-layouts: 32.1 us -> 5.66 us
  Pallas kernels: 239 us -> 219 us
    pallas_call x1, Pallas kernels: 239 us -> 219 us  [step(): pl.pallas_call(functools.partial(kernel, stages, micro, BLOCKS), out_shap...]
    unnamed x7, local copies, waits for them, and re-layouts: 21.1 us -> 5.66 us
    slice x1 -> x0, local copies, waits for them, and re-layouts: 5.6 us -> none  [step(): pairs[:, :, 1].reshape(1, d, ff)]
    reshape x1 -> x0, local copies, waits for them, and re-layouts: 5.35 us -> none  [step(): pairs = dgu.reshape(d, ff // LANES, 2, LANES)]
where the time goes in v2:
time: 225 us
  Pallas kernels  219 us (97%)
  local copies, waits for them, and re-layouts  5.66 us (3%)
    pallas_call x1, Pallas kernels, step(): pl.pallas_call(functools.partial(kernel, stages, micro, BLOCKS), out_shap...  219 us
    unnamed x7, local copies, waits for them, and re-layouts  5.66 us

profile of v2, /device:TPU:120, one launch (start us, length us, event | category | flops | bytes accessed | tf_op | source)
XLA Modules:
  0.0 225.0 jit_solution(15894187172328097635)
XLA Ops:
  0.6 218.6 %stage.1 = (bf16[1,512,1408]{2,1,0:T(8,128)(2,1)}, bf16[1,512,1408]{2,1,0:T(8,128)(2,1)}, bf16[1,1408,512]{2,1,0:T(8,128)(2,1)}, f32[32,256,2816]{2,1,0:T(8,128)}, bf16[32,256,1408]{2,1,0:T(8,128)(2,1)}) custom-call(bf16[32,256,512]{2,1,0:T(8,128)(2,1)} %bitcast.2, bf16[32,256,512]{2,1,0:T(8,128)(2,1)} %bitcast.3, bf16[1,512,1408]{2,1,0:T(8,128)(2,1)} %wg_ref.1, ...), custom_call_target="tpu_custom_call" | custom-call | tf_op jit(solution)/shard_map/stage/pallas_call | solution.py:318
  219.3 0.0 copy-start.1
  219.3 2.7 %copy.11 = bf16[1,512,1408]{2,1,0:T(8,128)(2,1)} copy(bf16[1,512,1408]{2,1,0:T(8,128)(2,1)} %get-tuple-element.12) | data formatting | bytes 2883584
  222.0 0.0 copy-done.1
  222.0 0.0 copy-start
  222.0 1.1 copy.12
  223.1 0.8 copy-done
  223.9 1.1 copy.13
Async XLA Ops:
  219.3 2.7 %copy-start.1 = (bf16[1,512,1408]{2,1,0:T(8,128)(2,1)S(1)}, bf16[1,512,1408]{2,1,0:T(8,128)(2,1)}, u32[]{:S(2)}) copy-start(bf16[1,512,1408]{2,1,0:T(8,128)(2,1)} %get-tuple-element.13) | copy-start | bytes 4325380
  222.0 1.9 copy-start

commit v3 on v2

v3 whole, which is shorter than its diff:
```python
import functools

import jax
import jax.numpy as jnp
from jax import lax
from jax.experimental import pallas as pl
from jax.experimental.pallas import tpu as pltpu
from jax.sharding import PartitionSpec as P

MESH = pl.DeviceIdType.MESH
F32, BF16 = jnp.float32, jnp.bfloat16
BLOCKS = 2
LANES = 128
AHEAD = (30, 26, 19, 16, 11, 9, 5, 1)
LAG = (4, 4, 12, 14, 19, 21, 32, 31)
SENDS = 4
IN, OUT = 3, 2
EPS = 1e-6


def dot(a, b):
    return jnp.dot(a, b, preferred_element_type=F32)


def kernel(
    stages, micro, blocks,
    x_ref, dy_ref, wg_ref, wu_ref, wd_ref, out_g, out_u, out_d, slopes_hbm, acts_hbm, dgus_hbm,
    wgu, wd, wgu_t, wd_t, hs, grads, fsend, bsend, slopes, acts, dgus, acts_in, dgus_in, turned, acc_gu, acc_d,
    w_sem, wd_sem, out_sem, recv_f, recv_b, send_f, send_b, put_s, put_a, put_d, get_s, get_a, get_d,
):
    me = lax.axis_index("pp")
    rows, d = hs.shape[1:]
    ff = wd.shape[0]
    first, last = me == 0, me == stages - 1
    pieces = ff // LANES
    wide = [(c, min(2 * LANES, ff - c)) for c in range(0, ff, 2 * LANES)]
    total_blocks = micro * blocks

    def x_copy(b):
        return pltpu.make_async_copy(x_ref.at[b], hs.at[b], recv_f.at[b])

    def dy_copy(b):
        return pltpu.make_async_copy(dy_ref.at[b], grads.at[b], recv_b.at[b])

    def f_copy(b):
        slot = lax.rem(b, SENDS)
        return pltpu.make_async_remote_copy(
            src_ref=fsend.at[slot], dst_ref=hs.at[b], send_sem=send_f.at[slot], recv_sem=recv_f.at[b],
            device_id={"pp": me + 1}, device_id_type=MESH,
        )

    def b_copy(b):
        slot = lax.rem(b, SENDS)
        return pltpu.make_async_remote_copy(
            src_ref=bsend.at[slot], dst_ref=grads.at[b], send_sem=send_b.at[slot], recv_sem=recv_b.at[b],
            device_id={"pp": me - 1}, device_id_type=MESH,
        )

    def put_slopes(b):
        slot = lax.rem(b, OUT)
        return pltpu.make_async_copy(slopes.at[IN + slot], slopes_hbm.at[b], put_s.at[slot])

    def put_acts(b):
        slot = lax.rem(b, OUT)
        return pltpu.make_async_copy(acts.at[slot], acts_hbm.at[b], put_a.at[slot])

    def put_dgus(b):
        slot = lax.rem(b, 2)
        return pltpu.make_async_copy(dgus.at[slot], dgus_hbm.at[b], put_d.at[slot])

    def get_slopes(b):
        slot = lax.rem(b, IN)
        return pltpu.make_async_copy(slopes_hbm.at[b], slopes.at[slot], get_s.at[slot])

    def get_terms(k):
        side = lax.rem(k, 2)
        copies = []
        for j in range(blocks):
            b = k * blocks + j
            copies.append(pltpu.make_async_copy(acts_hbm.at[b], acts_in.at[side, j], get_a.at[side, j]))
            copies.append(pltpu.make_async_copy(dgus_hbm.at[b], dgus_in.at[side, j], get_d.at[side, j]))
        return copies

    @pl.when(first)
    def _():
        x_copy(0).start()

    for c in range(pieces):
        at = pl.ds(c * LANES, LANES)
        pltpu.make_async_copy(wg_ref.at[0, :, at], wgu.at[:, pl.ds(2 * c * LANES, LANES)], w_sem).start()
        pltpu.make_async_copy(wu_ref.at[0, :, at], wgu.at[:, pl.ds((2 * c + 1) * LANES, LANES)], w_sem).start()
    pltpu.make_async_copy(wd_ref.at[0], wd, wd_sem).start()

    barrier = pltpu.get_barrier_semaphore()

    @pl.when(me > 0)
    def _():
        pl.semaphore_signal(barrier, inc=1, device_id={"pp": me - 1}, device_id_type=MESH)

    @pl.when(me < stages - 1)
    def _():
        pl.semaphore_signal(barrier, inc=1, device_id={"pp": me + 1}, device_id_type=MESH)

    @pl.when(first)
    def _():
        @pl.loop(1, total_blocks)
        def _(b):
            x_copy(b).start()

    @pl.when(last)
    def _():
        @pl.loop(0, total_blocks)
        def _(b):
            dy_copy(b).start()

    pltpu.make_async_copy(wgu, wgu, w_sem).wait()
    pltpu.make_async_copy(wd_ref.at[0], wd, wd_sem).wait()

    def turn_weights():
        acc_gu[...] = jnp.zeros_like(acc_gu)
        acc_d[...] = jnp.zeros_like(acc_d)
        for c in range(pieces):
            at = pl.ds(c * LANES, LANES)
            wd_t[:, at] = wd[at, :].T
        for c in range(2 * pieces):
            at = pl.ds(c * LANES, LANES)
            wgu_t[at, :] = wgu[:, at].T

    @pl.when(me > 0)
    def _():
        turn_weights()

    pl.semaphore_wait(barrier, jnp.where(first | last, 1, 2))

    def gated(gu, n):
        g = jnp.concatenate([gu[:, 2 * i * LANES:(2 * i + 1) * LANES] for i in range(n)], axis=1)
        u = jnp.concatenate([gu[:, (2 * i + 1) * LANES:(2 * i + 2) * LANES] for i in range(n)], axis=1)
        return g, u, 0.5 * jnp.tanh(0.5 * g) + 0.5

    def f_arrive(b):
        @pl.when(first)
        def _():
            x_copy(b).wait()

        @pl.when(me > 0)
        def _():
            f_copy(b).wait_recv()

        @pl.when(b >= OUT)
        def _():
            put_acts(b - OUT).wait()

        @pl.when((me < stages - 1) & (b >= OUT))
        def _():
            put_slopes(b - OUT).wait()

        @pl.when((me < stages - 1) & (b >= SENDS))
        def _():
            f_copy(b - SENDS).wait_send()

    def f_norm(b):
        h = hs[b].astype(F32)
        scale = lax.rsqrt(jnp.mean(h * h, -1, keepdims=True) + EPS)
        acts[lax.rem(b, OUT), :, ff:] = (h * scale).astype(BF16)

    def f_chunk(b, c, w, to):
        slot = lax.rem(b, OUT)
        gu = dot(acts[slot, :, ff:], wgu[:, 2 * c:2 * c + 2 * w])
        g, u, s = gated(gu, w // LANES)
        silu = g * s
        slopes[to, :, c:c + w] = silu
        slopes[to, :, ff + c:ff + c + w] = u * (s + silu * (1.0 - s))
        acts[slot, :, c:c + w] = (silu * u).astype(BF16)

    def f_out(b):
        y = dot(acts[lax.rem(b, OUT), :, :ff], wd[...]).astype(BF16)
        fsend[lax.rem(b, SENDS)] = (hs[b].astype(F32) + y.astype(F32)).astype(BF16)

    def forward(b):
        f_arrive(b)
        f_norm(b)
        to = jnp.where(last, lax.rem(b, IN), IN + lax.rem(b, OUT))
        for c, w in wide:
            f_chunk(b, c, w, to)
        f_out(b)

        @pl.when(me < stages - 1)
        def _():
            f_copy(b).start()
            put_slopes(b).start()

        put_acts(b).start()

    def b_arrive(b):
        @pl.when(last)
        def _():
            dy_copy(b).wait()

        @pl.when(me < stages - 1)
        def _():
            @pl.when(b + IN - 1 < total_blocks)
            def _():
                get_slopes(b + IN - 1).start()

            pltpu.make_async_remote_copy(
                src_ref=bsend.at[0], dst_ref=grads.at[b], send_sem=send_b.at[0], recv_sem=recv_b.at[b],
                device_id={"pp": me + 1}, device_id_type=MESH,
            ).wait_recv()
            get_slopes(b).wait()

        @pl.when(b >= 2)
        def _():
            put_dgus(b - 2).wait()

        @pl.when((me > 0) & (b >= SENDS))
        def _():
            b_copy(b - SENDS).wait_send()

    def b_chunk(b, c, w):
        slot, come = lax.rem(b, 2), lax.rem(b, IN)
        dact = dot(grads[b], wd_t[:, c:c + w]).astype(BF16).astype(F32)
        dgate = (dact * slopes[come, :, ff + c:ff + c + w]).astype(BF16)
        dup = (dact * slopes[come, :, c:c + w]).astype(BF16)
        for i in range(w // LANES):
            at = 2 * c + 2 * i * LANES
            dgus[slot, :, at:at + LANES] = dgate[:, i * LANES:(i + 1) * LANES]
            dgus[slot, :, at + LANES:at + 2 * LANES] = dup[:, i * LANES:(i + 1) * LANES]

    def b_out(b):
        da = dot(dgus[lax.rem(b, 2)], wgu_t[...]).astype(BF16).astype(F32)
        h = hs[b].astype(F32)
        scale = lax.rsqrt(jnp.mean(h * h, -1, keepdims=True) + EPS)
        pull = jnp.mean(da * h, -1, keepdims=True) * (scale * scale * scale)
        dh = (da * scale - h * pull).astype(BF16).astype(F32)
        bsend[lax.rem(b, SENDS)] = (grads[b].astype(F32) + dh).astype(BF16)

    def backward(b):
        b_arrive(b)
        for c, w in wide:
            b_chunk(b, c, w)
        b_out(b)

        @pl.when(me > 0)
        def _():
            b_copy(b).start()

        put_dgus(b).start()

    tokens = rows * blocks

    def weight(k):
        side = lax.rem(k, 2)

        @pl.when(k + 1 < micro)
        def _():
            for copy in get_terms(k + 1):
                copy.start()

        turned[1] = grads[pl.ds(k * blocks, blocks)].reshape(tokens, d).T
        for copy in get_terms(k):
            copy.wait()
        turned[0] = acts_in[side, :, :, ff:].reshape(tokens, d).T
        for c in range(0, 2 * ff, 2 * LANES):
            term = dot(turned[0], dgus_in[side, :, :, c:c + 2 * LANES].reshape(tokens, -1))
            acc_gu[:, c:c + 2 * LANES] += term.astype(BF16).astype(F32)
        for c, w in wide:
            term = dot(turned[1], acts_in[side, :, :, c:c + w].reshape(tokens, -1))
            acc_d[:, c:c + w] += term.astype(BF16).astype(F32)

    def mine(table):
        return sum(jnp.where(me == i, entry, 0) for i, entry in enumerate(table))

    ahead, lag = mine(AHEAD), mine(LAG)

    @pl.loop(0, total_blocks + max(a + b for a, b in zip(AHEAD, LAG)))
    def _(t):
        b = t - ahead
        late = b - lag

        @pl.when(first & (t == 2))
        def _():
            turn_weights()

        @pl.when((me < stages - 1) & (b == -1))
        def _():
            for i in range(IN - 1):
                get_slopes(i).start()

        @pl.when(t == total_blocks)
        def _():
            for i in range(OUT):
                put_acts(total_blocks - OUT + i).wait()

        @pl.when((me < stages - 1) & (t == total_blocks))
        def _():
            for i in range(OUT):
                put_slopes(total_blocks - OUT + i).wait()

        to_f, to_b = t < total_blocks, (b >= 0) & (b < total_blocks)

        @pl.when(to_b)
        def _():
            backward(b)

        @pl.when(b == total_blocks)
        def _():
            put_dgus(total_blocks - 2).wait()
            put_dgus(total_blocks - 1).wait()

        @pl.when(to_f)
        def _():
            forward(t)

        @pl.when(late == 0)
        def _():
            for copy in get_terms(0):
                copy.start()

        @pl.when((late >= 0) & (late < total_blocks) & (lax.rem(late, blocks) == blocks - 1))
        def _():
            weight(late // blocks)

    copies = []
    spare = micro % 2

    def out(src, dst):
        copies.append(pltpu.make_async_copy(src, dst, out_sem.at[len(copies)]))
        copies[-1].start()

    for j in range(blocks):
        at = slice(j * rows, (j + 1) * rows)
        for c in range(pieces):
            dgus_in[spare, j, :, c * LANES:(c + 1) * LANES] = acc_gu[at, 2 * c * LANES:(2 * c + 1) * LANES].astype(BF16)
            dgus_in[spare, j, :, ff + c * LANES:ff + (c + 1) * LANES] = acc_gu[at, (2 * c + 1) * LANES:(2 * c + 2) * LANES].astype(BF16)
        out(dgus_in.at[spare, j, :, pl.ds(0, ff)], out_g.at[0, pl.ds(j * rows, rows)])
        out(dgus_in.at[spare, j, :, pl.ds(ff, ff)], out_u.at[0, pl.ds(j * rows, rows)])
    for c in range(pieces):
        at = slice(c * LANES, (c + 1) * LANES)
        wd[at, :] = acc_d[:, at].astype(BF16).T
    out(wd, out_d.at[0])

    @pl.when(me < stages - 1)
    def _():
        @pl.loop(total_blocks - SENDS, total_blocks)
        def _(b):
            f_copy(b).wait_send()

    @pl.when(me > 0)
    def _():
        @pl.loop(total_blocks - SENDS, total_blocks)
        def _(b):
            b_copy(b).wait_send()

    for copy in copies:
        copy.wait()


def solution(mesh):
    stages = mesh.shape["pp"]

    def step(x, dy, w_gate, w_up, w_down):
        micro, tokens, d = x.shape
        ff = w_gate.shape[-1]
        rows = tokens // BLOCKS
        count = micro * BLOCKS
        any_space = pl.BlockSpec(memory_space=pl.ANY)
        out_g, out_u, out_d, *_ = pl.pallas_call(
            functools.partial(kernel, stages, micro, BLOCKS),
            out_shape=(
                jax.ShapeDtypeStruct((1, d, ff), BF16),
                jax.ShapeDtypeStruct((1, d, ff), BF16),
                jax.ShapeDtypeStruct((1, ff, d), BF16),
                jax.ShapeDtypeStruct((count, rows, 2 * ff), F32),
                jax.ShapeDtypeStruct((count, rows, ff + d), BF16),
                jax.ShapeDtypeStruct((count, rows, 2 * ff), BF16),
            ),
            in_specs=[any_space] * 5,
            out_specs=(any_space,) * 6,
            scratch_shapes=[
                pltpu.VMEM((d, 2 * ff), BF16),
                pltpu.VMEM((ff, d), BF16),
                pltpu.VMEM((2 * ff, d), BF16),
                pltpu.VMEM((d, ff), BF16),
                pltpu.VMEM((count, rows, d), BF16),
                pltpu.VMEM((count, rows, d), BF16),
                pltpu.VMEM((SENDS, rows, d), BF16),
                pltpu.VMEM((SENDS, rows, d), BF16),
                pltpu.VMEM((IN + OUT, rows, 2 * ff), F32),
                pltpu.VMEM((OUT, rows, ff + d), BF16),
                pltpu.VMEM((2, rows, 2 * ff), BF16),
                pltpu.VMEM((2, BLOCKS, rows, ff + d), BF16),
                pltpu.VMEM((2, BLOCKS, rows, 2 * ff), BF16),
                pltpu.VMEM((2, d, tokens), BF16),
                pltpu.VMEM((d, 2 * ff), F32),
                pltpu.VMEM((d, ff), F32),
                pltpu.SemaphoreType.DMA,
                pltpu.SemaphoreType.DMA,
                pltpu.SemaphoreType.DMA((2 * BLOCKS + 1,)),
                pltpu.SemaphoreType.DMA((count,)),
                pltpu.SemaphoreType.DMA((count,)),
                pltpu.SemaphoreType.DMA((SENDS,)),
                pltpu.SemaphoreType.DMA((SENDS,)),
                pltpu.SemaphoreType.DMA((OUT,)),
                pltpu.SemaphoreType.DMA((OUT,)),
                pltpu.SemaphoreType.DMA((2,)),
                pltpu.SemaphoreType.DMA((IN,)),
                pltpu.SemaphoreType.DMA((2, BLOCKS)),
                pltpu.SemaphoreType.DMA((2, BLOCKS)),
            ],
            compiler_params=pltpu.CompilerParams(collective_id=0, has_side_effects=True, vmem_limit_bytes=67_043_328),
            name="stage",
        )(x.reshape(count, rows, d), dy.reshape(count, rows, d), w_gate, w_up, w_down)
        return out_g, out_u, out_d

    return jax.shard_map(
        step,
        mesh=mesh,
        in_specs=(P("rep", None, None),) * 2 + (P("pp", None, None),) * 3,
        out_specs=(P(("rep", "pp"), None, None),) * 3,
        check_vma=False,
    )
```

time: 225 us -> 196 us (0.87); the launches traced: 225 us -> 193 us
  Pallas kernels: 219 us -> 187 us
    pallas_call x1, Pallas kernels: 219 us -> 187 us  [step(): pl.pallas_call(functools.partial(kernel, stages, micro, BLOCKS), out_shap...]
where the time goes in v3:
time: 196 us; the launch traced here: 193 us
  Pallas kernels  187 us (95%)
  local copies, waits for them, and re-layouts  5.66 us (3%)
    pallas_call x1, Pallas kernels, step(): pl.pallas_call(functools.partial(kernel, stages, micro, BLOCKS), out_shap...  187 us
    unnamed x7, local copies, waits for them, and re-layouts  5.66 us

profile of v3, /device:TPU:120, one launch (start us, length us, event | category | flops | bytes accessed | tf_op | source)
XLA Modules:
  0.0 193.3 jit_solution(12556123648736961474)
XLA Ops:
  0.6 187.0 %stage.1 = (bf16[1,512,1408]{2,1,0:T(8,128)(2,1)}, bf16[1,512,1408]{2,1,0:T(8,128)(2,1)}, bf16[1,1408,512]{2,1,0:T(8,128)(2,1)}, f32[32,256,2816]{2,1,0:T(8,128)...) custom-call(bf16[32,256,512]{2,1,0:T(8,128)(2,1)} %bitcast.2, bf16[32,256,512]{2,1,0:T(8,128)(2,1)} %bitcast.3, ...), custom_call_target="tpu_custom_call" | custom-call | tf_op jit(solution)/shard_map/stage/pallas_call | solution.py:367
  187.7 0.0 copy-start.1
  187.7 2.7 %copy.11 = bf16[1,512,1408]{2,1,0:T(8,128)(2,1)} copy(bf16[1,512,1408]{2,1,0:T(8,128)(2,1)} %get-tuple-element.12) | data formatting | bytes 2883584
  190.4 0.0 copy-done.1
  190.4 0.0 copy-start
  190.4 1.1 copy.12
  191.5 0.8 copy-done
  192.2 1.1 copy.13
Async XLA Ops:
  187.7 2.7 %copy-start.1 = (bf16[1,512,1408]{2,1,0:T(8,128)(2,1)S(1)}, bf16[1,512,1408]{2,1,0:T(8,128)(2,1)}, u32[]{:S(2)}) copy-start(bf16[1,512,1408]{2,1,0:T(8,128)(2,1)} %get-tuple-element.13) | copy-start | bytes 4325380
  190.4 1.9 copy-start

commit v4 on v3

--- a/solution.py
+++ b/solution.py
@@ -11,7 +11,7 @@
 F32, BF16 = jnp.float32, jnp.bfloat16
 BLOCKS = 2
 LANES = 128
-AHEAD = (30, 26, 19, 16, 11, 9, 5, 1)
+AHEAD = (30, 26, 19, 17, 12, 10, 5, 1)
 LAG = (4, 4, 12, 14, 19, 21, 32, 31)
 SENDS = 4
 IN, OUT = 3, 2
@@ -25,7 +25,7 @@
 def kernel(
     stages, micro, blocks,
     x_ref, dy_ref, wg_ref, wu_ref, wd_ref, out_g, out_u, out_d, slopes_hbm, acts_hbm, dgus_hbm,
-    wgu, wd, wgu_t, wd_t, hs, grads, fsend, bsend, slopes, acts, dgus, acts_in, dgus_in, turned, acc_gu, acc_d,
+    wgu, wd, wgu_t, wd_t, hs, grads, fsend, bsend, slopes, acts, dgus, acts_in, dgus_in, normed, acc_gu, acc_d,
     w_sem, wd_sem, out_sem, recv_f, recv_b, send_f, send_b, put_s, put_a, put_d, get_s, get_a, get_d,
 ):
     me = lax.axis_index("pp")
@@ -158,14 +158,24 @@
         def _():
             f_copy(b - SENDS).wait_send()
 
+    def turned(block):
+        return jnp.concatenate([block[:, c:c + rows].T for c in range(0, d, rows)], axis=1)
+
+    def upright(parts):
+        return jnp.concatenate(
+            [jnp.concatenate([part[:, c:c + rows] for part in parts], axis=1) for c in range(0, d, rows)], axis=0
+        )
+
     def f_norm(b):
         h = hs[b].astype(F32)
         scale = lax.rsqrt(jnp.mean(h * h, -1, keepdims=True) + EPS)
-        acts[lax.rem(b, OUT), :, ff:] = (h * scale).astype(BF16)
+        a = (h * scale).astype(BF16)
+        normed[...] = a
+        acts[lax.rem(b, OUT), :, ff:] = turned(a)
 
     def f_chunk(b, c, w, to):
         slot = lax.rem(b, OUT)
-        gu = dot(acts[slot, :, ff:], wgu[:, 2 * c:2 * c + 2 * w])
+        gu = dot(normed[...], wgu[:, 2 * c:2 * c + 2 * w])
         g, u, s = gated(gu, w // LANES)
         silu = g * s
         slopes[to, :, c:c + w] = silu
@@ -233,6 +243,7 @@
         pull = jnp.mean(da * h, -1, keepdims=True) * (scale * scale * scale)
         dh = (da * scale - h * pull).astype(BF16).astype(F32)
         bsend[lax.rem(b, SENDS)] = (grads[b].astype(F32) + dh).astype(BF16)
+        hs[b] = turned(grads[b])
 
     def backward(b):
         b_arrive(b)
@@ -256,15 +267,15 @@
             for copy in get_terms(k + 1):
                 copy.start()
 
-        turned[1] = grads[pl.ds(k * blocks, blocks)].reshape(tokens, d).T
         for copy in get_terms(k):
             copy.wait()
-        turned[0] = acts_in[side, :, :, ff:].reshape(tokens, d).T
+        a_t = upright([acts_in[side, j, :, ff:] for j in range(blocks)])
+        dy_t = upright([hs[k * blocks + j] for j in range(blocks)])
         for c in range(0, 2 * ff, 2 * LANES):
-            term = dot(turned[0], dgus_in[side, :, :, c:c + 2 * LANES].reshape(tokens, -1))
+            term = dot(a_t, dgus_in[side, :, :, c:c + 2 * LANES].reshape(tokens, -1))
             acc_gu[:, c:c + 2 * LANES] += term.astype(BF16).astype(F32)
         for c, w in wide:
-            term = dot(turned[1], acts_in[side, :, :, c:c + w].reshape(tokens, -1))
+            term = dot(dy_t, acts_in[side, :, :, c:c + w].reshape(tokens, -1))
             acc_d[:, c:c + w] += term.astype(BF16).astype(F32)
 
     def mine(table):
@@ -353,6 +364,25 @@
 
     for copy in copies:
         copy.wait()
+
+
+def place(g_ref, u_ref, d_ref, out_g, out_u, out_d, buf_g, buf_u, buf_d, sem_in, sem_out):
+    moves = []
+    for ref, buf, out in ((g_ref, buf_g, out_g), (u_ref, buf_u, out_u), (d_ref, buf_d, out_d)):
+        rows = ref.shape[1] // 4
+        for i in range(4):
+            at, n = pl.ds(i * rows, rows), len(moves)
+            moves.append((
+                pltpu.make_async_copy(ref.at[0, at], buf.at[at], sem_in.at[n]),
+                pltpu.make_async_copy(buf.at[at], out.at[0, at], sem_out.at[n]),
+            ))
+    for come, _ in moves:
+        come.start()
+    for come, go in moves:
+        come.wait()
+        go.start()
+    for _, go in moves:
+        go.wait()
 
 
 def solution(mesh):
@@ -390,7 +420,7 @@
                 pltpu.VMEM((2, rows, 2 * ff), BF16),
                 pltpu.VMEM((2, BLOCKS, rows, ff + d), BF16),
                 pltpu.VMEM((2, BLOCKS, rows, 2 * ff), BF16),
-                pltpu.VMEM((2, d, tokens), BF16),
+                pltpu.VMEM((rows, d), BF16),
                 pltpu.VMEM((d, 2 * ff), F32),
                 pltpu.VMEM((d, ff), F32),
                 pltpu.SemaphoreType.DMA,
@@ -410,7 +440,19 @@
             compiler_params=pltpu.CompilerParams(collective_id=0, has_side_effects=True, vmem_limit_bytes=67_043_328),
             name="stage",
         )(x.reshape(count, rows, d), dy.reshape(count, rows, d), w_gate, w_up, w_down)
-        return out_g, out_u, out_d
+        results = (out_g, out_u, out_d)
+        return pl.pallas_call(
+            place,
+            out_shape=tuple(jax.ShapeDtypeStruct(r.shape, r.dtype) for r in results),
+            in_specs=[any_space] * 3,
+            out_specs=(any_space,) * 3,
+            scratch_shapes=[
+                *(pltpu.VMEM(r.shape[1:], r.dtype) for r in results),
+                pltpu.SemaphoreType.DMA((12,)),
+                pltpu.SemaphoreType.DMA((12,)),
+            ],
+            name="place",
+        )(*results)
 
     return jax.shard_map(
         step,

time: 196 us -> 186 us (0.949); the launches traced: 193 us -> 186 us
  local copies, waits for them, and re-layouts: 5.66 us -> 0 us
    unnamed x7 -> x0, local copies, waits for them, and re-layouts: 5.66 us -> none
    pallas_call x1, Pallas kernels: 187 us -> 182 us  [step(): pl.pallas_call(functools.partial(kernel, stages, micro, BLOCKS), out_shap...]
    pallas_call x0 -> x1, Pallas kernels: none -> 3.86 us  [step(): pl.pallas_call(place, out_shape=tuple((jax.ShapeDtypeStruct(r.shape, r.dt...]
where the time goes in v4:
time: 186 us
  Pallas kernels  186 us (100%)
    pallas_call x1, Pallas kernels, step(): pl.pallas_call(functools.partial(kernel, stages, micro, BLOCKS), out_shap...  182 us
    pallas_call x1, Pallas kernels, step(): pl.pallas_call(place, out_shape=tuple((jax.ShapeDtypeStruct(r.shape, r.dt...  3.86 us

profile of v4, /device:TPU:120, one launch (start us, length us, event | category | flops | bytes accessed | tf_op | source)
XLA Modules:
  0.0 186.1 jit_solution(4280646268239824154)
XLA Ops:
  0.6 181.7 %stage.1 = (bf16[1,512,1408]{2,1,0:T(8,128)(2,1)}, bf16[1,512,1408]{2,1,0:T(8,128)(2,1)}, bf16[1,1408,512]{2,1,0:T(8,128)(2,1)}, f32[32,256,2816]{2,1,0:T(8,128)...) custom-call(bf16[32,256,512]{2,1,0:T(8,128)(2,1)} %bitcast.2, bf16[32,256,512]{2,1,0:T(8,128)(2,1)} %bitcast.3, ...), custom_call_target="tpu_custom_call" | custom-call | tf_op jit(solution)/shard_map/stage/pallas_call | solution.py:397
  182.3 3.9 %place.1 = (bf16[1,512,1408]{2,1,0:T(8,128)(2,1)}, bf16[1,512,1408]{2,1,0:T(8,128)(2,1)}, bf16[1,1408,512]{2,1,0:T(8,128)(2,1)}) custom-call(bf16[1,512,1408]{2,1,0:T(8,128)(2,1)} %get-tuple-element.6.g_ref, bf16[1,512,1408]{2,1,0:T(8,128)(2,1)} %get-tuple-element.7.u_ref, bf16[1,1408,512]{2,1,0:T(8,128)(2,1)} %get-tuple-element.8.d_ref), custom_call_target="tpu_custom_call" | custom-call | tf_op jit(solution)/shard_map/place/pallas_call | solution.py:444
